TPU v7x, 32 devices: a whole 2x2x4 slice. The times are simulated.
32 devices in a mesh: groups: 2 (over x), tensor: 16 (over z, y, core).
Axes of the slice: x: 2, y: 2, z: 4, core: 2. Of those that a mesh axis runs over, the one named last changes fastest.
Arguments:
- stem_field: float32 [8, 2, 262144], P('groups', None, 'tensor'), parts along dimension 0, may hold values from -6 to 6
- branches: float32 [4, 2, 2, 256, 256], P(None, None, None, None, 'tensor'), may hold values from -0.25 to 0.25
- branch_order: int32 [4], replicated, may hold values from 0 to 3, each once
- slice_values: int32 [8, 4], P('groups'), parts along dimension 0, may hold values from 0 to 1
Outputs:
- amplitudes: float32 [4, 262144], P('groups', 'tensor'), parts along dimension 0
There are 2 independent parts, one for each index of `groups`. A program takes and returns all parts, laid end to end along the dimension named above; an argument that names none is the same for every part. Nothing has to cross between parts.
Inputs may be any that keep to these rules, and one draw needn't show every extreme that they name: `branch_order`: each branch is merged exactly once.
All inputs are finite; a program needn't handle non-finite values.
Results may differ from a plain program's by a relative error of at most 0.00014.
Values sent between devices are 32-bit elements; how exact they have to be, the bound alone decides.
A program may use at most 64 MiB of HBM per device.

v0:
```python
import jax
import jax.numpy as jnp
from jax import lax
from jax.sharding import PartitionSpec as P

STEPS = 4


def product(left, right):
    return jnp.einsum("smi,sil->slm", left, right, precision=lax.Precision.HIGHEST)


def select_table(branch_now, values_now):
    return jnp.where(
        (values_now == 1)[:, None, None, None], branch_now[1][None], branch_now[0][None]
    )


def combine_branch(stem_part, branch_now, values_now):
    batch_rows = stem_part.shape[0]
    contract_width = branch_now.shape[2]
    middle = stem_part.shape[2] // contract_width
    blocks = stem_part.reshape(batch_rows, 2, middle, contract_width)
    chosen = select_table(branch_now, values_now)
    real_part = product(blocks[:, 0], chosen[:, 0]) - product(blocks[:, 1], chosen[:, 1])
    imag_part = product(blocks[:, 0], chosen[:, 1]) + product(blocks[:, 1], chosen[:, 0])
    return jnp.stack([real_part, imag_part], axis=1)


def split_rows(combined, shards):
    batch_rows, parts, contract_width, middle = combined.shape
    return combined.reshape(batch_rows, parts, shards, contract_width // shards, middle)


def per_device(stem_field, branches, branch_order, slice_values):
    shards = lax.axis_size("tensor")
    tables = [
        lax.all_gather(
            lax.dynamic_index_in_dim(branches, branch_order[step_index], 0, keepdims=False),
            "tensor",
            axis=3,
            tiled=True,
        )
        for step_index in range(STEPS)
    ]
    current = stem_field
    for step_index in range(STEPS):
        combined = combine_branch(current, tables[step_index], slice_values[:, step_index])
        reindexed = lax.all_to_all(
            split_rows(combined, shards), "tensor", split_axis=2, concat_axis=2, tiled=True
        )
        current = reindexed.reshape(current.shape)
    amplitudes = jnp.sum(current, axis=0)
    return amplitudes


def solution(mesh):
    return jax.shard_map(
        per_device,
        mesh=mesh,
        in_specs=(
            P("groups", None, "tensor"),
            P(None, None, None, None, "tensor"),
            P(),
            P("groups", None),
        ),
        out_specs=P("groups", "tensor"),
        check_vma=False,
    )
```

profile of v0, /device:TPU:0, one launch (start us, length us, event | category | flops | bytes accessed | tf_op | source)
XLA Modules:
  0.0 263.2 jit_solution(7321279914040590710)
XLA Ops:
  6.5 1.5 fusion.12
  15.4 1.6 constant_dynamic-slice_fusion
  17.1 0.7 all-gather.15.cloned.1.call-update
  18.6 1.0 fusion.11
  19.6 1.5 reshape.74
  21.1 36.7 %all-gather.13.cloned.1.call-done = f32[1,2,2,256,256]{3,4,2,1,0:T(8,128)} async-done(((f32[1,2,2,256,16]{3,4,2,1,0:T(8,128)}), f32[1,2,2,256,256]{3,4,2,1,0:T(8,128)}) %all-gather.13.cloned.1.call-update) | async-done | bytes 1048592 | tf_op jit(solution)/shard_map/all_gather | solution.py:38
  57.8 1.3 slice_bitcast_fusion.27
  59.3 1.0 copy.87
  60.3 36.5 %all-gather.15.cloned.1.call-done = f32[1,2,2,256,256]{3,4,2,1,0:T(8,128)} async-done(((f32[1,2,2,256,16]{3,4,2,1,0:T(8,128)}), f32[1,2,2,256,256]{3,4,2,1,0:T(8,128)}) %all-gather.15.cloned.1.call-update) | async-done | bytes 1048592 | tf_op jit(solution)/shard_map/all_gather | solution.py:38
  96.9 1.3 slice_bitcast_fusion.25
  98.1 1.0 copy.88
  99.1 1.0 copy.89
  100.1 1.7 broadcast_select_fusion
  101.8 0.8 fusion.3
  103.2 0.8 convolution_subtract_fusion.3
  104.0 1.0 copy.91
  105.0 2.0 fusion.4
  107.0 2.0 convolution_add_fusion.3
  109.1 1.0 copy.92
  110.1 1.3 copy_bitcast_fusion.3
  111.4 1.5 reshape.79
  112.9 3.7 %all-to-all-start = ((f32[16,1,8192]{2,1,0:T(1,128)}), f32[16,1,8192]{2,1,0:T(1,128)S(1)}, u32[]{:S(2)}, u32[]{:S(2)}) async-start(f32[16,1,8192]{2,1,0:T(1,128)} %reshape.79), calls=%async_computation | async-start | bytes 1048576 | tf_op jit(solution)/shard_map/all_to_all | solution.py:49
  117.2 16.7 %all-to-all-done = f32[16,1,8192]{2,1,0:T(1,128)S(1)} async-done(((f32[16,1,8192]{2,1,0:T(1,128)}), f32[16,1,8192]{2,1,0:T(1,128)S(1)}, u32[]{:S(2)}, u32[]{:S(2)}) %all-to-all-start) | async-done | bytes 524320 | tf_op jit(solution)/shard_map/all_to_all | solution.py:49
  134.4 2.8 %reduce.9 = f32[16,8192]{1,0:T(8,128)} reduce(f32[16,1,8192]{2,1,0:T(1,128)S(1)} %all-to-all-done, f32[]{:T(128)} %broadcast.33), dimensions={1}, to_apply=%all_to_all.12.reduce_sub_computation | reduce | bytes 1048580 | tf_op jit(solution)/shard_map/all_to_all | solution.py:49
  137.2 1.5 reshape.80
  138.6 1.1 copy.94
  139.8 1.5 reshape_reshape.9
  141.3 0.8 fusion.2
  142.1 0.8 convolution_subtract_fusion.2
  143.1 0.8 fusion.5
  143.9 0.8 convolution_add_fusion.2
  145.1 1.4 reshape.81
  146.5 5.4 %all-to-all-start.1 = ((f32[16,1,8192]{2,1,0:T(1,128)}), f32[16,1,8192]{2,1,0:T(1,128)S(1)}, u32[]{:S(2)}, u32[]{:S(2)}) async-start(f32[16,1,8192]{2,1,0:T(1,128)} %reshape.81), calls=%async_computation.1 | async-start | bytes 1048576 | tf_op jit(solution)/shard_map/all_to_all | solution.py:49
  151.9 1.3 slice_bitcast_fusion.31
  153.4 1.0 copy.83
  154.4 24.6 %all-gather.11.cloned.1.call-done = f32[1,2,2,256,256]{3,4,2,1,0:T(8,128)} async-done(((f32[1,2,2,256,16]{3,4,2,1,0:T(8,128)}), f32[1,2,2,256,256]{3,4,2,1,0:T(8,128)}) %all-gather.11.cloned.1.call-update) | async-done | bytes 1048592 | tf_op jit(solution)/shard_map/all_gather | solution.py:38
  179.1 1.3 slice_bitcast_fusion.29
  180.3 1.0 copy.84
  181.4 1.0 copy.85
  182.4 3.3 %broadcast_select_fusion.2 = (f32[4,2,256,256]{3,2,0,1:T(8,128)}, f32[4,2,256,256]{3,2,0,1:T(8,128)S(1)}) fusion(f32[2,256,256]{2,1,0:T(8,128)} %copy.85, f32[2,256,256]{2,1,0:T(8,128)} %copy.84, pred[4]{0:T(512)(128)(4,1)S(1)} %get-tuple-element.6, f32[2,256,256]{2,1,0:T(8,128)} %copy.83, f32[2,256,256]{2,1,0:T(8,128)S(1)} %copy.82, ...), kind=kLoop, calls=%fused_computation.22 | loop fusion | flops 1048576 | bytes 6291464 | tf_op jit(solution)/shard_map/jit(_where)/select_n | solution.py:14
  185.6 2.8 %reduce.10 = f32[16,8192]{1,0:T(8,128)} reduce(f32[16,1,8192]{2,1,0:T(1,128)S(1)} %all-to-all-done.1, f32[]{:T(128)} %broadcast.33), dimensions={1}, to_apply=%all_to_all.13.reduce_sub_computation | reduce | bytes 1048580 | tf_op jit(solution)/shard_map/all_to_all | solution.py:49
  188.4 1.5 reshape.82
  189.9 1.1 copy.98
  191.0 1.5 reshape_reshape.10
  192.5 2.2 fusion.1
  194.7 2.0 fusion.6
  196.7 0.8 convolution_subtract_fusion.1
  197.5 1.0 copy.99
  198.5 2.0 convolution_add_fusion.1
  200.6 1.0 copy.100
  201.6 1.3 copy_bitcast_fusion.1
  202.9 1.4 reshape.83
  204.3 18.0 %all_to_all.20 = f32[16,1,8192]{2,1,0:T(1,128)S(1)} all-to-all(f32[16,1,8192]{2,1,0:T(1,128)} %reshape.83), channel_id=1, replica_groups=mesh['groups'=2,'tensor'=16] {'tensor'}, dimensions={0} | all-to-all | bytes 1048576 | tf_op jit(solution)/shard_map/all_to_all | solution.py:49
  222.3 2.8 %reduce.11 = f32[16,8192]{1,0:T(8,128)} reduce(f32[16,1,8192]{2,1,0:T(1,128)S(1)} %all_to_all.20, f32[]{:T(128)} %broadcast.33), dimensions={1}, to_apply=%all_to_all.14.reduce_sub_computation | reduce | bytes 1048580 | tf_op jit(solution)/shard_map/all_to_all | solution.py:49
  225.1 1.5 reshape.84
  226.5 1.1 copy.102
  227.6 1.5 reshape_reshape.11
  229.1 0.8 fusion
  229.9 1.5 fusion.7
  231.4 0.8 convolution_subtract_fusion
  232.5 1.8 convolution_add_fusion
  235.2 18.2 %all_to_all.21 = f32[16,1,8192]{2,1,0:T(1,128)S(1)} all-to-all(f32[16,1,8192]{2,1,0:T(1,128)S(1)} %reshape.85), channel_id=1, replica_groups=mesh['groups'=2,'tensor'=16] {'tensor'}, dimensions={0} | all-to-all | bytes 1048576 | tf_op jit(solution)/shard_map/all_to_all | solution.py:49
  253.5 1.9 reduce.12
  255.9 0.8 reduce_sum.12
  (26 shorter events, 5.0 us)
Async XLA Ops:
  6.5 51.3 %all-gather.13.cloned.1.call-start = ((), (), s32[]{:S(2)}) async-start(), calls=%async_computation.6 | async-start | bytes 1114112 | tf_op jit(solution)/shard_map/all_gather | solution.py:38
  17.1 79.8 %all-gather.15.cloned.1.call-start = ((), (), s32[]{:S(2)}) async-start(), calls=%async_computation.7 | async-start | bytes 1114112 | tf_op jit(solution)/shard_map/all_gather | solution.py:38
  17.8 134.1 %all-gather.9.cloned.1.call-start = ((), (), s32[]{:S(2)}) async-start(), calls=%async_computation.4 | async-start | bytes 1114112 | tf_op jit(solution)/shard_map/all_gather | solution.py:38
  101.8 1.3 copy-start.1
  112.9 21.0 %all-to-all-start = ((f32[16,1,8192]{2,1,0:T(1,128)}), f32[16,1,8192]{2,1,0:T(1,128)S(1)}, u32[]{:S(2)}, u32[]{:S(2)}) async-start(f32[16,1,8192]{2,1,0:T(1,128)} %reshape.79), calls=%async_computation | async-start | bytes 1048576 | tf_op jit(solution)/shard_map/all_to_all | solution.py:49
  116.6 62.5 %all-gather.11.cloned.1.call-start = ((), (), s32[]{:S(2)}) async-start(), calls=%async_computation.5 | async-start | bytes 1114112 | tf_op jit(solution)/shard_map/all_gather | solution.py:38
  146.5 39.1 %all-to-all-start.1 = ((f32[16,1,8192]{2,1,0:T(1,128)}), f32[16,1,8192]{2,1,0:T(1,128)S(1)}, u32[]{:S(2)}, u32[]{:S(2)}) async-start(f32[16,1,8192]{2,1,0:T(1,128)} %reshape.81), calls=%async_computation.1 | async-start | bytes 1048576 | tf_op jit(solution)/shard_map/all_to_all | solution.py:49
  192.5 4.2 %copy-start = (f32[4,2,256,256]{3,2,0,1:T(8,128)S(1)}, f32[4,2,256,256]{3,2,0,1:T(8,128)}, u32[]{:S(2)}) copy-start(f32[4,2,256,256]{3,2,0,1:T(8,128)} %get-tuple-element.27) | copy-start | bytes 6291460
Sparse Core Ops, SparseCore 0:
  17.2 40.5 all-gather.12
  60.0 36.8 all-gather.14
  99.1 37.8 all-gather.8
  139.0 40.0 all-gather.10
where the time goes:
time: 265 us; the launch traced here: 263 us
  waiting for transfers between devices  117 us (44%)
  local copies, waits for them, and re-layouts  40.4 us (15%)
  blocking collectives  36.2 us (14%)
  matrix products  20.9 us (8%)
  between operations  20.8 us (8%)
  other arithmetic  19.3 us (7%)
  starting transfers between devices  9.16 us (3%)
    all_gather x4, waiting for transfers between devices, per_device(): lax.all_gather(lax.dynamic_index_in_dim(branches, branch_order[step_index...  97.9 us
    all_to_all x2, blocking collectives, per_device(): lax.all_to_all(split_rows(combined, shards), 'tensor', split_axis=2, conc...  36.2 us
    dot_general x16, matrix products, product(): jnp.einsum('smi,sil->slm', left, right, precision=lax.Precision.HIGHEST)  20.9 us
    all_to_all x2, waiting for transfers between devices, per_device(): lax.all_to_all(split_rows(combined, shards), 'tensor', split_axis=2, conc...  16.7 us
    broadcast_in_dim x12, local copies, waits for them, and re-layouts, select_table(): jnp.where((values_now == 1)[:, None, None, None], branch_now[1][None], br...  11.5 us
    unnamed x12, local copies, waits for them, and re-layouts  10.3 us
    all_to_all x4, other arithmetic, per_device(): lax.all_to_all(split_rows(combined, shards), 'tensor', split_axis=2, conc...  10.2 us
    all_to_all x2, starting transfers between devices, per_device(): lax.all_to_all(split_rows(combined, shards), 'tensor', split_axis=2, conc...  9.04 us
  transfers between devices with their start and end apart: 6, of which 4 were waited for; matrix products, arithmetic and copies ran while one was open for 16% of the time, Pallas kernels for 0%

commit v1 on v0

v1 whole, which is shorter than its diff:
```python
import functools

import jax
import jax.numpy as jnp
from jax import lax
from jax.experimental import pallas as pl
from jax.experimental.pallas import tpu as pltpu
from jax.sharding import PartitionSpec as P

MESH = pl.DeviceIdType.MESH


def product(left, right):
    return jnp.einsum("smi,sil->slm", left, right, precision=lax.Precision.HIGHEST)


def combine_branch(stem_part, branch_now, values_now):
    slices, _, _, width = stem_part.shape
    chosen = jnp.where(
        (values_now == 1)[:, None, None, None], branch_now[1][None], branch_now[0][None]
    )
    real_part = product(stem_part[:, 0], chosen[:, 0]) - product(stem_part[:, 1], chosen[:, 1])
    imag_part = product(stem_part[:, 0], chosen[:, 1]) + product(stem_part[:, 1], chosen[:, 0])
    return jnp.stack([real_part, imag_part], axis=1)


def plain_device(stem_field, branches, branch_order, slice_values):
    shards = lax.axis_size("tensor")
    steps = branches.shape[0]
    width = branches.shape[3]
    current = stem_field
    for step in range(steps):
        table = lax.all_gather(
            lax.dynamic_index_in_dim(branches, branch_order[step], 0, keepdims=False),
            "tensor",
            axis=3,
            tiled=True,
        )
        slices, parts, entries = current.shape
        blocks = current.reshape(slices, parts, entries // width, width)
        combined = combine_branch(blocks, table, slice_values[:, step])
        combined = combined.reshape(slices, parts, shards, width // shards, entries // width)
        current = lax.all_to_all(
            combined, "tensor", split_axis=2, concat_axis=2, tiled=True
        ).reshape(current.shape)
    return jnp.sum(current, axis=0)


def split(value):
    high = value.astype(jnp.bfloat16)
    return high, (value - high.astype(jnp.float32)).astype(jnp.bfloat16)


def kernel(cfg, values, stem, shard, out, g0, g1, g2, g3, w, y, sent, got, fsent,
           ring_sem, pair_sem, side_sem, cross_sem, send_sem, x_sem, f_sem, xs_sem, fs_sem):
    T, S, K, CB, M, CLO, CHI = cfg
    chips = T // 2
    zs = chips // 2
    gs = (g0, g1, g2, g3)
    gx = lax.axis_index("groups")
    me = lax.axis_index("tensor")
    core = lax.rem(me, 2)
    col = lax.rem(me // 2, 2)
    depth = me // 4
    pos = jnp.where(col == 0, depth, chips - 1 - depth)

    def at(position, which):
        p = lax.rem(position + 2 * chips, chips)
        z = jnp.where(p < zs, p, chips - 1 - p)
        c = jnp.where(p < zs, 0, 1)
        return (z * 2 + c) * 2 + which

    right, left = at(pos + 1, core), at(pos - 1, core)
    partner = me + 1 - 2 * core

    barrier = pltpu.get_barrier_semaphore()
    for d in range(1, T):
        pl.semaphore_signal(barrier, inc=1, device_id=(gx, lax.rem(me + d, T)), device_id_type=MESH)
    pl.semaphore_signal(barrier, inc=1, device_id=(1 - gx, me), device_id_type=MESH)
    pl.semaphore_wait(barrier, T)

    started = []

    def push(src, dst, ssem, rsem, device):
        copy = pltpu.make_async_remote_copy(
            src_ref=src, dst_ref=dst, send_sem=ssem, recv_sem=rsem,
            device_id=device, device_id_type=MESH,
        )
        copy.start()
        return copy

    counter = [0] * 4
    own_part = pl.ds(gx, 3)

    def hop(t, rel, to, device):
        n = counter[t]
        counter[t] += 1
        src = (shard.at[t] if rel == 0 else gs[t].at[0, rel]).at[own_part]
        started.append(push(src, gs[t].at[0, to].at[own_part], send_sem.at[t, n],
                            ring_sem.at[t, to], (gx, device)))

    def pair(t, rel):
        n = counter[t]
        counter[t] += 1
        if rel == 0:
            src, dst = shard.at[t], gs[t].at[1, 0]
        else:
            src, dst = gs[t].at[0, rel].at[own_part], gs[t].at[1, rel].at[own_part]
        started.append(push(src, dst, send_sem.at[t, n], pair_sem.at[t, rel], (gx, partner)))

    def await_ring(t, rel):
        dst = gs[t].at[0, rel].at[own_part]
        pltpu.make_async_remote_copy(
            src_ref=dst, dst_ref=dst, send_sem=ring_sem.at[t, rel], recv_sem=ring_sem.at[t, rel],
            device_id=(gx, right), device_id_type=MESH).wait_recv()

    def begin(t):
        hop(t, 0, chips - 1, right)
        hop(t, 0, 1, left)
        pair(t, 0)

    def advance(t, k):
        half = chips // 2
        if k < half:
            rel = chips - k
            await_ring(t, rel)
            if k < half - 1 or t % 2 == 0:
                hop(t, rel, rel - 1, right)
            pair(t, rel)
            await_ring(t, k)
            if k < half - 1 or t % 2 == 1:
                hop(t, k, k + 1, left)
            pair(t, k)
        else:
            await_ring(t, half)
            pair(t, half)
            n = counter[t]
            counter[t] += 1
            lane = gs[t].at[0, pl.ds(1, chips - 1), gx * 3]
            started.append(push(lane, lane, send_sem.at[t, n], side_sem.at[t], (1 - gx, me)))

    def finish(t):
        lane = gs[t].at[0, pl.ds(1, chips - 1), (1 - gx) * 3]
        pltpu.make_async_remote_copy(
            src_ref=lane, dst_ref=lane, send_sem=side_sem.at[t], recv_sem=side_sem.at[t],
            device_id=(1 - gx, me), device_id_type=MESH).wait_recv()
        n = counter[t]
        counter[t] += 1
        there = gs[t].at[1, pl.ds(1, chips - 1), (1 - gx) * 3]
        started.append(push(lane, there, send_sem.at[t, n], cross_sem.at[t], (gx, partner)))

    def settle(t):
        for rel in range(chips):
            dst = gs[t].at[1, 0] if rel == 0 else gs[t].at[1, rel].at[own_part]
            pltpu.make_async_remote_copy(
                src_ref=dst, dst_ref=dst, send_sem=pair_sem.at[t, rel], recv_sem=pair_sem.at[t, rel],
                device_id=(gx, partner), device_id_type=MESH).wait_recv()
        there = gs[t].at[1, pl.ds(1, chips - 1), (1 - gx) * 3]
        pltpu.make_async_remote_copy(
            src_ref=there, dst_ref=there, send_sem=cross_sem.at[t], recv_sem=cross_sem.at[t],
            device_id=(gx, partner), device_id_type=MESH).wait_recv()

    def load_tables(t):
        g = gs[t]
        for a in range(T):
            z, c, which = a // 4, (a // 2) % 2, a % 2
            apos = z if c == 0 else chips - 1 - z
            rel = lax.rem(apos - pos + chips, chips)
            other = jnp.where(core == which, 0, 1)
            mine = jnp.logical_and(rel == 0, other == 0)
            for v in range(2):
                for p in range(2):
                    block = jnp.where(mine, shard[t, 2 * v + p], g[other, rel, 2 * v + p])
                    high, low = split(block)
                    rows = slice(a * K, (a + 1) * K)
                    cols = slice(p * CB, (p + 1) * CB)
                    w[v, 0, rows, cols] = high
                    w[v, 1, rows, cols] = low

    def merge(v, real, imag):
        rh, rl = split(real)
        ih, il = split(imag)
        ah = jnp.concatenate([jnp.concatenate([rh, -ih], axis=1), jnp.concatenate([ih, rh], axis=1)], axis=0)
        al = jnp.concatenate([jnp.concatenate([rl, -il], axis=1), jnp.concatenate([il, rl], axis=1)], axis=0)
        dims = (((1,), (1,)), ((), ()))
        dot = functools.partial(lax.dot_general, dimension_numbers=dims,
                                preferred_element_type=jnp.float32)
        wh, wl = w[v, 0], w[v, 1]
        return dot(wh, ah) + (dot(wh, al) + dot(wl, ah))

    def regroup(ref, chi_major):
        rows = CB // CLO
        pieces = []
        for lo in range(CLO):
            if chi_major:
                pieces.append(jnp.concatenate(
                    [ref[pl.ds(c * CLO + lo, T, stride=K), :] for c in range(CHI)], axis=0))
            else:
                pieces.append(ref[pl.ds(lo, rows, stride=CLO), :])
        return [jnp.concatenate([b[:, p * M:(p + 1) * M] for b in pieces], axis=1) for p in range(2)]

    for t in range(4):
        begin(t)
    for k in range(1, chips // 2 + 1):
        for t in range(4):
            advance(t, k)
    for t in range(4):
        finish(t)

    settle(0)
    load_tables(0)
    for s in range(S):
        y[s] = merge(values[s, 0], stem[s, 0], stem[s, 1])
    settle(1)
    load_tables(1)
    for s in range(S):
        real, imag = regroup(y.at[s], True)
        r = merge(values[s, 1], real, imag)
        for a in range(T):
            sent[pl.ds((a * S + s) * K, K), :] = r[a * K:(a + 1) * K]
    span = S * K
    block_of = lambda i: pl.ds(pl.multiple_of(i * span, span), span)
    copies = []
    for d in range(1, T):
        to = lax.rem(me + d, T)
        copies.append(push(sent.at[block_of(to)], got.at[block_of(me)], xs_sem.at[d], x_sem.at[d], (gx, to)))
    got[block_of(me), :] = sent[block_of(me), :]
    settle(2)
    load_tables(2)
    for d in range(1, T):
        frm = lax.rem(me - d + T, T)
        dst = got.at[block_of(frm)]
        pltpu.make_async_remote_copy(
            src_ref=dst, dst_ref=dst, send_sem=x_sem.at[d], recv_sem=x_sem.at[d],
            device_id=(gx, frm), device_id_type=MESH).wait_recv()
    sums = [None, None]
    for s in range(S):
        parts = [[], []]
        for hi in range(CHI):
            block = jnp.concatenate(
                [got[pl.ds(s * K + hi * CLO + lo, T, stride=span), :] for lo in range(CLO)], axis=0)
            turned = block.T
            for p in range(2):
                parts[p].append(jnp.concatenate(
                    [turned[(p * CHI + c) * T:(p * CHI + c + 1) * T] for c in range(CHI)], axis=1))
        real, imag = [jnp.concatenate(q, axis=0) for q in parts]
        r = merge(values[s, 2], real, imag)
        one = values[s, 3] == 1
        for v in range(2):
            part = jnp.where(one if v else jnp.logical_not(one), r, 0.0)
            sums[v] = part if s == 0 else sums[v] + part
    y[0] = sums[0]
    y[1] = sums[1]
    settle(3)
    load_tables(3)
    total = None
    for v in range(2):
        real, imag = regroup(y.at[v], False)
        r = merge(v, real, imag)
        total = r if v == 0 else total + r
    fsent[...] = total
    row_of = lambda i: pl.ds(pl.multiple_of(i * K, K), K)
    for d in range(1, T):
        to = lax.rem(me + d, T)
        copies.append(push(fsent.at[row_of(to)], out.at[row_of(me)], fs_sem.at[d], f_sem.at[d], (gx, to)))
    out[row_of(me), :] = fsent[row_of(me), :]
    for d in range(1, T):
        frm = lax.rem(me - d + T, T)
        dst = out.at[row_of(frm)]
        pltpu.make_async_remote_copy(
            src_ref=dst, dst_ref=dst, send_sem=f_sem.at[d], recv_sem=f_sem.at[d],
            device_id=(gx, frm), device_id_type=MESH).wait_recv()
    for copy in started + copies:
        copy.wait_send()


def fused_device(stem_field, branches, branch_order, slice_values):
    T = lax.axis_size("tensor")
    S, _, entries = stem_field.shape
    steps, _, _, CB, K = branches.shape
    M = entries // CB
    CLO = CB // M
    CHI = K // CLO
    stem = stem_field.reshape(S, 2, M, CB)
    shard = jnp.take(branches, branch_order, axis=0).reshape(steps, 4, CB, K).transpose(0, 1, 3, 2)
    third = shard[2].reshape(4, K, CLO, T, CHI).transpose(0, 1, 4, 2, 3).reshape(4, K, CB)
    fourth = shard[3].reshape(4, K, CLO, T, CHI).transpose(0, 1, 2, 4, 3).reshape(4, K, CB)
    shard = jnp.stack([shard[0], shard[1], third, fourth])
    vmem = pl.BlockSpec(memory_space=pltpu.VMEM)
    dma = pltpu.SemaphoreType.DMA
    table = pltpu.VMEM((2, T // 2, 4, K, CB), jnp.float32)
    moved = pltpu.VMEM((T * S * K, 2 * M), jnp.float32)
    gathered = pl.pallas_call(
        functools.partial(kernel, (T, S, K, CB, M, CLO, CHI)),
        out_shape=jax.ShapeDtypeStruct((T * K, 2 * M), jnp.float32),
        in_specs=[pl.BlockSpec(memory_space=pltpu.SMEM), vmem, vmem],
        out_specs=vmem,
        scratch_shapes=[
            table, table, table, table,
            pltpu.VMEM((2, 2, CB, 2 * CB), jnp.bfloat16),
            pltpu.VMEM((S, CB, 2 * M), jnp.float32),
            moved, moved,
            pltpu.VMEM((CB, 2 * M), jnp.float32),
            dma((4, T // 2)), dma((4, T // 2)), dma((4,)), dma((4,)),
            dma((4, 20)),
            dma((T,)), dma((T,)), dma((T,)), dma((T,)),
        ],
        compiler_params=pltpu.CompilerParams(collective_id=0, has_side_effects=True),
    )(slice_values, stem, shard)
    ordered = gathered.reshape(T, K, 2, T, CHI).transpose(2, 3, 1, 0, 4)
    return ordered.reshape(2, entries)


def solution(mesh):
    def per_device(stem_field, branches, branch_order, slice_values):
        shards = lax.axis_size("tensor")
        steps, _, _, width, columns = branches.shape
        middle = stem_field.shape[2] // width
        fits = (
            mesh.shape["groups"] == 2 and shards % 8 == 0 and columns % 8 == 0 and steps == 4
            and 2 * middle == 128 and width % middle == 0 and columns % (width // middle) == 0
        )
        run = fused_device if fits else plain_device
        return run(stem_field, branches, branch_order, slice_values)

    return jax.shard_map(
        per_device,
        mesh=mesh,
        in_specs=(
            P("groups", None, "tensor"),
            P(None, None, None, None, "tensor"),
            P(),
            P("groups", None),
        ),
        out_specs=P("groups", "tensor"),
        check_vma=False,
    )
```

time: 265 us -> 77.6 us (0.29)
  waiting for transfers between devices: 117 us -> 0 us
  Pallas kernels: 0 us -> 58.6 us
  blocking collectives: 36.2 us -> 0 us
  local copies, waits for them, and re-layouts: 40.4 us -> 16.5 us
  matrix products: 20.9 us -> 0 us
  between operations: 20.8 us -> 0.09 us
  other arithmetic: 19.3 us -> 2.17 us
  starting transfers between devices: 9.16 us -> 0 us
    all_gather x4 -> x0, waiting for transfers between devices: 97.9 us -> none  [per_device(): lax.all_gather(lax.dynamic_index_in_dim(branches, branch_order[step_index...]
    pallas_call x0 -> x1, Pallas kernels: none -> 58.6 us  [fused_device(): pl.pallas_call(functools.partial(kernel, (T, S, K, CB, M, CLO, CHI)), out...]
    all_to_all x2 -> x0, blocking collectives: 36.2 us -> none  [per_device(): lax.all_to_all(split_rows(combined, shards), 'tensor', split_axis=2, conc...]
    dot_general x16 -> x0, matrix products: 20.9 us -> none  [product(): jnp.einsum('smi,sil->slm', left, right, precision=lax.Precision.HIGHEST)]
    all_to_all x2 -> x0, waiting for transfers between devices: 16.7 us -> none  [per_device(): lax.all_to_all(split_rows(combined, shards), 'tensor', split_axis=2, conc...]
    broadcast_in_dim x12 -> x0, local copies, waits for them, and re-layouts: 11.5 us -> none  [select_table(): jnp.where((values_now == 1)[:, None, None, None], branch_now[1][None], br...]
    unnamed x12 -> x4, local copies, waits for them, and re-layouts: 10.3 us -> 0.01 us
    all_to_all x4 -> x0, other arithmetic: 10.2 us -> none  [per_device(): lax.all_to_all(split_rows(combined, shards), 'tensor', split_axis=2, conc...]
  transfers between devices with their start and end apart: 6 -> 0, of which waited for: 4 -> 0; matrix products, arithmetic and copies ran while one was open for 16% -> 0% of each run, Pallas kernels for 0% -> 0%
where the time goes in v1:
time: 77.6 us; the launch traced here: 77.4 us
  Pallas kernels  58.6 us (76%)
  local copies, waits for them, and re-layouts  16.5 us (21%)
  other arithmetic  2.17 us (3%)
    pallas_call x1, Pallas kernels, fused_device(): pl.pallas_call(functools.partial(kernel, (T, S, K, CB, M, CLO, CHI)), out...  58.6 us
    reshape x1, local copies, waits for them, and re-layouts, fused_device(): return ordered.reshape(2, entries)  6.65 us
    transpose x1, local copies, waits for them, and re-layouts, fused_device(): ordered = gathered.reshape(T, K, 2, T, CHI).transpose(2, 3, 1, 0, 4)  4.7 us

profile of v1, /device:TPU:0, one launch (start us, length us, event | category | flops | bytes accessed | tf_op | source)
XLA Modules:
  0.0 77.4 jit_solution(2239401028490411651)
XLA Ops:
  0.0 0.0 copy-start
  0.0 0.7 compare_and_fusion
  0.7 0.7 compare_select_fusion
  1.4 0.0 copy-done
  1.4 0.6 gather_fusion
  2.0 0.1 select_bitcast_fusion
  2.1 0.2 copy.8
  2.3 0.0 copy-start.1
  2.3 0.3 copy.9
  2.6 0.4 stack_reshape.6
  3.1 0.2 copy.10
  3.3 0.4 copy.11
  3.6 0.4 stack_reshape.7
  4.1 0.7 pad_maximum_fusion.shard
  4.8 0.0 copy-done.1
  4.8 1.2 %reshape.16.stem = f32[4,2,64,256]{3,2,1,0:T(8,128)} reshape(f32[4,2,16384]{2,1,0:T(2,128)S(1)} %copy-done.1) | data formatting | bytes 1048576 | tf_op jit(solution)/shard_map/reshape | solution.py:284
  6.0 58.6 %shard_map.46 = f32[256,128]{1,0:T(8,128)} custom-call(s32[4,4]{1,0:T(4,128)} %values.1, f32[4,2,64,256]{3,2,1,0:T(8,128)} %reshape.16.stem, f32[4,4,16,256]{3,2,1,0:T(8,128)} %pad_maximum_fusion.shard), custom_call_target="tpu_custom_call" | custom-call | tf_op jit(solution)/shard_map/pallas_call | solution.py:293
  64.7 1.0 %copy.12 = f32[256,128]{0,1:T(8,128)S(1)} copy(f32[256,128]{1,0:T(8,128)} %shard_map.46) | data formatting | bytes 262144 | tf_op jit(solution)/shard_map/pallas_call | solution.py:293
  65.7 0.3 reshape.17
  66.0 4.7 %copy.13 = f32[2,16,16,16,4]{4,3,2,1,0:T(8,128)} copy(f32[2,16,16,16,4]{2,3,4,1,0:T(8,128)S(1)} %bitcast.15) | data formatting | bytes 262144 | tf_op jit(solution)/shard_map/transpose | solution.py:310
  70.7 6.7 %reshape.18 = f32[2,16384]{1,0:T(2,128)} reshape(f32[2,16,16,16,4]{4,3,2,1,0:T(8,128)} %copy.13) | data formatting | bytes 262144 | tf_op jit(solution)/shard_map/reshape | solution.py:311
  (3 shorter events, 0.0 us)
Async XLA Ops:
  0.0 1.4 %copy-start = (f32[4,2,2,256,16]{3,4,2,1,0:T(8,128)S(1)}, f32[4,2,2,256,16]{3,4,2,1,0:T(8,128)}, u32[]{:S(2)}) copy-start(f32[4,2,2,256,16]{3,4,2,1,0:T(8,128)} %param.5) | copy-start | bytes 786436
  2.3 2.5 %copy-start.1 = (f32[4,2,16384]{2,1,0:T(2,128)S(1)}, f32[4,2,16384]{2,1,0:T(2,128)}, u32[]{:S(2)}) copy-start(f32[4,2,16384]{2,1,0:T(2,128)} %param.4) | copy-start | bytes 1572868

commit v2 on v1

v2 whole, which is shorter than its diff:
```python
import functools

import jax
import jax.numpy as jnp
from jax import lax
from jax.experimental import pallas as pl
from jax.experimental.pallas import tpu as pltpu
from jax.sharding import PartitionSpec as P

MESH = pl.DeviceIdType.MESH


def product(left, right):
    return jnp.einsum("smi,sil->slm", left, right, precision=lax.Precision.HIGHEST)


def combine_branch(stem_part, branch_now, values_now):
    slices, _, _, width = stem_part.shape
    chosen = jnp.where(
        (values_now == 1)[:, None, None, None], branch_now[1][None], branch_now[0][None]
    )
    real_part = product(stem_part[:, 0], chosen[:, 0]) - product(stem_part[:, 1], chosen[:, 1])
    imag_part = product(stem_part[:, 0], chosen[:, 1]) + product(stem_part[:, 1], chosen[:, 0])
    return jnp.stack([real_part, imag_part], axis=1)


def plain_device(stem_field, branches, branch_order, slice_values):
    shards = lax.axis_size("tensor")
    steps = branches.shape[0]
    width = branches.shape[3]
    current = stem_field
    for step in range(steps):
        table = lax.all_gather(
            lax.dynamic_index_in_dim(branches, branch_order[step], 0, keepdims=False),
            "tensor",
            axis=3,
            tiled=True,
        )
        slices, parts, entries = current.shape
        blocks = current.reshape(slices, parts, entries // width, width)
        combined = combine_branch(blocks, table, slice_values[:, step])
        combined = combined.reshape(slices, parts, shards, width // shards, entries // width)
        current = lax.all_to_all(
            combined, "tensor", split_axis=2, concat_axis=2, tiled=True
        ).reshape(current.shape)
    return jnp.sum(current, axis=0)


def split(value):
    high = value.astype(jnp.bfloat16)
    return high, (value - high.astype(jnp.float32)).astype(jnp.bfloat16)


def kernel(cfg, values, stem, shard, out, g0, g1, g2, g3, w0, w1, w2, w3, y, sent, got, fsent, fgot, turned_f,
           ring_sem, pair_sem, side_sem, cross_sem, send_sem, x_sem, f_sem, xs_sem, fs_sem):
    T, S, K, CB, M, CLO, CHI = cfg
    chips = T // 2
    half = chips // 2
    zs = chips // 2
    gs = (g0, g1, g2, g3)
    ws = (w0, w1, w2, w3)
    gx = lax.axis_index("groups")
    me = lax.axis_index("tensor")
    core = lax.rem(me, 2)
    col = lax.rem(me // 2, 2)
    depth = me // 4
    pos = jnp.where(col == 0, depth, chips - 1 - depth)

    def at(position, which):
        p = lax.rem(position + 2 * chips, chips)
        z = jnp.where(p < zs, p, chips - 1 - p)
        c = jnp.where(p < zs, 0, 1)
        return (z * 2 + c) * 2 + which

    right, left = at(pos + 1, core), at(pos - 1, core)
    partner = me + 1 - 2 * core

    barrier = pltpu.get_barrier_semaphore()
    for d in range(1, T):
        pl.semaphore_signal(barrier, inc=1, device_id=(gx, lax.rem(me + d, T)), device_id_type=MESH)
    pl.semaphore_signal(barrier, inc=1, device_id=(1 - gx, me), device_id_type=MESH)
    pl.semaphore_wait(barrier, T)

    started = []
    counter = [0] * 4
    own_part = pl.ds(gx, 3)
    out_part = gx * 3
    in_part = (1 - gx) * 3

    def push(src, dst, ssem, rsem, device):
        copy = pltpu.make_async_remote_copy(
            src_ref=src, dst_ref=dst, send_sem=ssem, recv_sem=rsem,
            device_id=device, device_id_type=MESH,
        )
        copy.start()
        started.append(copy)

    def arrived(dst, rsem):
        pltpu.make_async_remote_copy(
            src_ref=dst, dst_ref=dst, send_sem=rsem, recv_sem=rsem,
            device_id=(gx, partner), device_id_type=MESH).wait_recv()

    def token(t):
        counter[t] += 1
        return send_sem.at[t, counter[t] - 1]

    def hop(t, rel, to, device):
        src = (shard.at[t] if rel == 0 else gs[t].at[0, rel]).at[own_part]
        push(src, gs[t].at[0, to].at[own_part], token(t), ring_sem.at[t, to], (gx, device))

    def spread(t, rel):
        src = gs[t].at[0, rel]
        push(src.at[out_part], src.at[out_part], token(t), side_sem.at[t, rel], (1 - gx, me))
        push(src.at[own_part], gs[t].at[1, rel].at[own_part], token(t), pair_sem.at[t, rel], (gx, partner))

    def cross(t, rel):
        src = gs[t].at[0, rel].at[in_part]
        arrived(src, side_sem.at[t, rel])
        push(src, gs[t].at[1, rel].at[in_part], token(t), cross_sem.at[t, rel], (gx, partner))

    def begin(t):
        hop(t, 0, chips - 1, right)
        hop(t, 0, 1, left)
        push(shard.at[t], gs[t].at[1, 0], token(t), pair_sem.at[t, 0], (gx, partner))

    def advance(t, k):
        if k < half:
            rel = chips - k
            arrived(gs[t].at[0, rel].at[own_part], ring_sem.at[t, rel])
            if k < half - 1 or t % 2 == 0:
                hop(t, rel, rel - 1, right)
            spread(t, rel)
            arrived(gs[t].at[0, k].at[own_part], ring_sem.at[t, k])
            if k < half - 1 or t % 2 == 1:
                hop(t, k, k + 1, left)
            spread(t, k)
        else:
            arrived(gs[t].at[0, half].at[own_part], ring_sem.at[t, half])
            spread(t, half)
        if k > 1:
            cross(t, chips - k + 1)
            cross(t, k - 1)
        if k == half:
            cross(t, half)

    def settle(t):
        arrived(gs[t].at[1, 0], pair_sem.at[t, 0])
        for rel in range(1, chips):
            arrived(gs[t].at[1, rel].at[own_part], pair_sem.at[t, rel])
            arrived(gs[t].at[1, rel].at[in_part], cross_sem.at[t, rel])

    def load_tables(t):
        settle(t)
        g, w = gs[t], ws[t]
        for a in range(T):
            z, c, which = a // 4, (a // 2) % 2, a % 2
            apos = z if c == 0 else chips - 1 - z
            rel = lax.rem(apos - pos + chips, chips)
            other = jnp.where(core == which, 0, 1)
            for v in range(2):
                for p in range(2):
                    high, low = split(g[other, rel, 2 * v + p])
                    rows = slice(a * K, (a + 1) * K)
                    cols = slice(p * CB, (p + 1) * CB)
                    w[v, 0, rows, cols] = high
                    w[v, 1, rows, cols] = low
        if t >= 2 and CHI > 1:
            row = lax.broadcasted_iota(jnp.int32, (CB, CB), 0)
            lane = lax.broadcasted_iota(jnp.int32, (CB, CB), 1)
            if t == 2:
                c, lo, h = lane // (CLO * T), (lane // T) % CLO, lane % T
            else:
                lo, c, h = lane // (CHI * T), (lane // T) % CHI, lane % T
            move = (row == (lo * T + h) * CHI + c).astype(jnp.float32).astype(jnp.bfloat16)
            for v in range(2):
                for i in range(2):
                    for p in range(2):
                        cols = slice(p * CB, (p + 1) * CB)
                        w[v, i, :, cols] = jnp.dot(
                            w[v, i, :, cols], move, preferred_element_type=jnp.float32
                        ).astype(jnp.bfloat16)

    def merge(t, v, real, imag):
        rh, rl = split(real)
        ih, il = split(imag)
        ah = jnp.concatenate([jnp.concatenate([rh, -ih], axis=1), jnp.concatenate([ih, rh], axis=1)], axis=0)
        al = jnp.concatenate([jnp.concatenate([rl, -il], axis=1), jnp.concatenate([il, rl], axis=1)], axis=0)
        dims = (((1,), (1,)), ((), ()))
        dot = functools.partial(lax.dot_general, dimension_numbers=dims,
                                preferred_element_type=jnp.float32)
        wh, wl = ws[t][v, 0], ws[t][v, 1]
        return dot(wh, ah) + (dot(wh, al) + dot(wl, ah))

    def regroup(ref, chi_major):
        rows = CB // CLO
        pieces = []
        for lo in range(CLO):
            if chi_major:
                pieces.append(jnp.concatenate(
                    [ref[pl.ds(c * CLO + lo, T, stride=K), :] for c in range(CHI)], axis=0))
            else:
                pieces.append(ref[pl.ds(lo, rows, stride=CLO), :])
        return [jnp.concatenate([b[:, p * M:(p + 1) * M] for b in pieces], axis=1) for p in range(2)]

    order = sorted(((t, k) for t in range(4) for k in range(half + 1)), key=lambda i: (i[1] + 1.1 * i[0], i[0]))
    pending = []
    for item in order:
        if item[1] == 0:
            begin(item[0])
        elif item == (0, half):
            advance(*item)
            break
        else:
            advance(*item)
    pending = list(order[order.index((0, half)) + 1:])

    def more(count=1):
        for _ in range(count):
            if pending:
                t, k = pending.pop(0)
                if k == 0:
                    begin(t)
                else:
                    advance(t, k)

    for t in range(4):
        gs[t][0, 0] = shard[t]
    load_tables(0)
    for s in range(S):
        y[s] = merge(0, values[s, 0], stem[s, 0], stem[s, 1])
        more()
    while any(t == 1 for t, k in pending):
        more()
    load_tables(1)
    rows_of = lambda s, i: pl.ds(pl.multiple_of((s * T + i) * K, K), K)
    for s in range(S):
        real, imag = regroup(y.at[s], True)
        sent[pl.ds(s * T * K, T * K), :] = merge(1, values[s, 1], real, imag)
        for d in range(1, T):
            to = lax.rem(me + d, T)
            push(sent.at[rows_of(s, to)], got.at[rows_of(s, me)], xs_sem.at[s, d], x_sem.at[s, d], (gx, to))
        got[rows_of(s, me), :] = sent[rows_of(s, me), :]
        more()
    more(len(pending))
    load_tables(2)
    load_tables(3)
    sums = [None, None]
    for s in range(S):
        for d in range(1, T):
            frm = lax.rem(me - d + T, T)
            arrived(got.at[rows_of(s, frm)], x_sem.at[s, d])
        parts = [[], []]
        for hi in range(CHI):
            block = jnp.concatenate(
                [got[pl.ds(s * T * K + hi * CLO + lo, T, stride=K), :] for lo in range(CLO)], axis=0)
            turned = block.T
            for p in range(2):
                parts[p].append(jnp.concatenate(
                    [turned[(p * CHI + c) * T:(p * CHI + c + 1) * T] for c in range(CHI)], axis=1))
        real, imag = [jnp.concatenate(q, axis=0) for q in parts]
        r = merge(2, values[s, 2], real, imag)
        one = values[s, 3] == 1
        for v in range(2):
            part = jnp.where(one if v else jnp.logical_not(one), r, 0.0)
            sums[v] = part if s == 0 else sums[v] + part
    y[0] = sums[0]
    y[1] = sums[1]
    total = None
    for v in range(2):
        real, imag = regroup(y.at[v], False)
        r = merge(3, v, real, imag)
        total = r if v == 0 else total + r
    fsent[...] = total
    row_of = lambda i: pl.ds(pl.multiple_of(i * K, K), K)
    for d in range(1, T):
        to = lax.rem(me + d, T)
        push(fsent.at[row_of(to)], fgot.at[row_of(me)], fs_sem.at[d], f_sem.at[d], (gx, to))
    fgot[row_of(me), :] = fsent[row_of(me), :]
    for d in range(1, T):
        frm = lax.rem(me - d + T, T)
        arrived(fgot.at[row_of(frm)], f_sem.at[d])

    lanes = 2 * M
    width = lanes // CHI
    across = jnp.concatenate([fgot[pl.ds(c, T, stride=K), :] for c in range(K)], axis=0)
    halves = CB // lanes
    for i in range(halves):
        turned_f[i] = across[i * lanes:(i + 1) * lanes].T
    pieces = [jnp.concatenate(
        [turned_f[i, pl.ds(c, 2 * T, stride=CHI), :] for i in range(halves)], axis=1) for c in range(CHI)]
    count = CB // width
    lined = jnp.concatenate(
        [jnp.concatenate([q[:, j * width:(j + 1) * width] for q in pieces], axis=1) for j in range(count)], axis=0)
    row = lax.broadcasted_iota(jnp.int32, (lanes, lanes), 0)
    lane = lax.broadcasted_iota(jnp.int32, (lanes, lanes), 1)
    move = (row == (lane % CHI) * width + lane // CHI).astype(jnp.float32).astype(jnp.bfloat16)
    first, rest = lined.astype(jnp.bfloat16), lined
    rest = rest - first.astype(jnp.float32)
    second, third = split(rest)
    dot = functools.partial(jnp.dot, preferred_element_type=jnp.float32)
    placed = (dot(first, move) + dot(second, move)) + dot(third, move)
    for j in range(count):
        out[:, j * lanes:(j + 1) * lanes] = placed[j * 2 * T:(j + 1) * 2 * T]
    for copy in started:
        copy.wait_send()


def fused_device(stem_field, branches, branch_order, slice_values):
    T = lax.axis_size("tensor")
    S, _, entries = stem_field.shape
    steps, _, _, CB, K = branches.shape
    M = entries // CB
    CLO = CB // M
    CHI = K // CLO
    stem = stem_field.reshape(S, 2, M, CB)
    shard = jnp.take(branches, branch_order, axis=0).reshape(steps, 4, CB, K).transpose(0, 1, 3, 2)
    vmem = pl.BlockSpec(memory_space=pltpu.VMEM)
    dma = pltpu.SemaphoreType.DMA
    table = pltpu.VMEM((2, T // 2, 4, K, CB), jnp.float32)
    merged = pltpu.VMEM((2, 2, CB, 2 * CB), jnp.bfloat16)
    moved = pltpu.VMEM((T * S * K, 2 * M), jnp.float32)
    gathered = pl.pallas_call(
        functools.partial(kernel, (T, S, K, CB, M, CLO, CHI)),
        out_shape=jax.ShapeDtypeStruct((2 * T, entries // T), jnp.float32),
        in_specs=[pl.BlockSpec(memory_space=pltpu.SMEM), vmem, vmem],
        out_specs=vmem,
        scratch_shapes=[
            table, table, table, table,
            merged, merged, merged, merged,
            pltpu.VMEM((S, CB, 2 * M), jnp.float32),
            moved, moved,
            pltpu.VMEM((CB, 2 * M), jnp.float32),
            pltpu.VMEM((CB, 2 * M), jnp.float32),
            pltpu.VMEM((CB // (2 * M), 2 * M, 2 * M), jnp.float32),
            dma((4, T // 2)), dma((4, T // 2)), dma((4, T // 2)), dma((4, T // 2)),
            dma((4, 2 * T + 2)),
            dma((S, T)), dma((T,)), dma((S, T)), dma((T,)),
        ],
        compiler_params=pltpu.CompilerParams(collective_id=0, has_side_effects=True),
    )(slice_values, stem, shard)
    return gathered.reshape(2, entries)


def solution(mesh):
    def per_device(stem_field, branches, branch_order, slice_values):
        shards = lax.axis_size("tensor")
        steps, _, _, width, columns = branches.shape
        middle = stem_field.shape[2] // width
        fits = (
            mesh.shape["groups"] == 2 and shards % 8 == 0 and columns % 8 == 0 and steps == 4
            and 2 * middle == 128 and width % middle == 0 and columns % (width // middle) == 0
        )
        run = fused_device if fits else plain_device
        return run(stem_field, branches, branch_order, slice_values)

    return jax.shard_map(
        per_device,
        mesh=mesh,
        in_specs=(
            P("groups", None, "tensor"),
            P(None, None, None, None, "tensor"),
            P(),
            P("groups", None),
        ),
        out_specs=P("groups", "tensor"),
        check_vma=False,
    )
```

time: 77.6 us -> 70.1 us (0.903)
  local copies, waits for them, and re-layouts: 16.5 us -> 3.82 us
  Pallas kernels: 58.6 us -> 63.9 us
    transpose x3 -> x0, local copies, waits for them, and re-layouts: 5.4 us -> none  [the longest x1 4.7 us: fused_device(): ordered = gathered.reshape(T, K, 2, T, CHI).transpose(2, 3, 1, 0, 4)]
    reshape x2 -> x1, local copies, waits for them, and re-layouts: 6.97 us -> 1.67 us  [fused_device(): return gathered.reshape(2, entries)]
    pallas_call x1, Pallas kernels: 58.6 us -> 63.9 us  [fused_device(): pl.pallas_call(functools.partial(kernel, (T, S, K, CB, M, CLO, CHI)), out...]
    pallas_call x1 -> x0, local copies, waits for them, and re-layouts: 1 us -> none  [fused_device(): pl.pallas_call(functools.partial(kernel, (T, S, K, CB, M, CLO, CHI)), out...]
    another operation x2 -> x0, local copies, waits for them, and re-layouts: 0.85 us -> none  [fused_device(): shard = jnp.stack([shard[0], shard[1], third, fourth])]
where the time goes in v2:
time: 70.1 us; the launch traced here: 69.9 us
  Pallas kernels  63.9 us (91%)
  local copies, waits for them, and re-layouts  3.82 us (5%)
  other arithmetic  2.15 us (3%)
    pallas_call x1, Pallas kernels, fused_device(): pl.pallas_call(functools.partial(kernel, (T, S, K, CB, M, CLO, CHI)), out...  63.9 us
    reshape x1, local copies, waits for them, and re-layouts, fused_device(): return gathered.reshape(2, entries)  1.67 us

profile of v2, /device:TPU:0, one launch (start us, length us, event | category | flops | bytes accessed | tf_op | source)
XLA Modules:
  0.0 69.9 jit_solution(15630961733098466816)
XLA Ops:
  0.0 0.0 copy-start
  0.0 0.7 %compare_and_fusion = pred[4]{0:T(512)(128)(4,1)S(1)} fusion(s32[4]{0:T(128)} %param.6), kind=kLoop, calls=%fused_computation.4 | loop fusion | flops 24 | bytes 20 | tf_op jit(solution)/shard_map/jit(_take)/and | solution.py:316
  0.7 0.7 compare_select_fusion
  1.4 0.0 copy-done
  1.4 0.6 gather_fusion
  2.0 0.0 copy-start.1
  2.0 0.8 %select_bitcast_fusion.shard = f32[4,4,16,256]{3,2,1,0:T(8,128)} fusion(f32[4,4,256,16]{2,3,1,0:T(8,128)S(1)} %bitcast.3, pred[4]{0:T(512)(128)(4,1)S(1)} %compare_and_fusion), kind=kLoop, calls=%fused_computation.1 | loop fusion | flops 65536 | bytes 524292 | tf_op jit(solution)/shard_map/transpose | solution.py:316
  2.7 0.4 copy-done.1
  3.1 1.2 %reshape.13.stem = f32[4,2,64,256]{3,2,1,0:T(8,128)} reshape(f32[4,2,16384]{2,1,0:T(2,128)S(1)} %copy-done.1) | data formatting | bytes 1048576 | tf_op jit(solution)/shard_map/reshape | solution.py:315
  4.3 63.9 %shard_map.46 = f32[32,1024]{1,0:T(8,128)} custom-call(s32[4,4]{1,0:T(4,128)} %values.1, f32[4,2,64,256]{3,2,1,0:T(8,128)} %reshape.13.stem, f32[4,4,16,256]{3,2,1,0:T(8,128)} %select_bitcast_fusion.shard), custom_call_target="tpu_custom_call" | custom-call | tf_op jit(solution)/shard_map/pallas_call | solution.py:322
  68.2 1.7 %reshape.14 = f32[2,16384]{1,0:T(2,128)} reshape(f32[32,1024]{1,0:T(8,128)} %shard_map.46) | data formatting | bytes 262144 | tf_op jit(solution)/shard_map/reshape | solution.py:341
  (1 shorter events, 0.0 us)
Async XLA Ops:
  0.0 1.4 %copy-start = (f32[4,2,2,256,16]{3,4,2,1,0:T(8,128)S(1)}, f32[4,2,2,256,16]{3,4,2,1,0:T(8,128)}, u32[]{:S(2)}) copy-start(f32[4,2,2,256,16]{3,4,2,1,0:T(8,128)} %param.5) | copy-start | bytes 786436
  2.0 1.1 %copy-start.1 = (f32[4,2,16384]{2,1,0:T(2,128)S(1)}, f32[4,2,16384]{2,1,0:T(2,128)}, u32[]{:S(2)}) copy-start(f32[4,2,16384]{2,1,0:T(2,128)} %param.4) | copy-start | bytes 1572868

commit v3 on v2

--- a/solution.py
+++ b/solution.py
@@ -52,11 +52,9 @@
 
 
 def kernel(cfg, values, stem, shard, out, g0, g1, g2, g3, w0, w1, w2, w3, y, sent, got, fsent, fgot, turned_f,
-           ring_sem, pair_sem, side_sem, cross_sem, send_sem, x_sem, f_sem, xs_sem, fs_sem):
+           gather_sem, send_sem, x_sem, f_sem, xs_sem, fs_sem):
     T, S, K, CB, M, CLO, CHI = cfg
-    chips = T // 2
-    half = chips // 2
-    zs = chips // 2
+    Z = T // 4
     gs = (g0, g1, g2, g3)
     ws = (w0, w1, w2, w3)
     gx = lax.axis_index("groups")
@@ -64,16 +62,8 @@
     core = lax.rem(me, 2)
     col = lax.rem(me // 2, 2)
     depth = me // 4
-    pos = jnp.where(col == 0, depth, chips - 1 - depth)
-
-    def at(position, which):
-        p = lax.rem(position + 2 * chips, chips)
-        z = jnp.where(p < zs, p, chips - 1 - p)
-        c = jnp.where(p < zs, 0, 1)
-        return (z * 2 + c) * 2 + which
-
-    right, left = at(pos + 1, core), at(pos - 1, core)
     partner = me + 1 - 2 * core
+    across_y = me + 2 - 4 * col
 
     barrier = pltpu.get_barrier_semaphore()
     for d in range(1, T):
@@ -83,9 +73,9 @@
 
     started = []
     counter = [0] * 4
-    own_part = pl.ds(gx, 3)
-    out_part = gx * 3
-    in_part = (1 - gx) * 3
+    ours = pl.ds(2 * gx, 2)
+    theirs = pl.ds(2 - 2 * gx, 2)
+    far = pl.ds(1, Z - 1)
 
     def push(src, dst, ssem, rsem, device):
         copy = pltpu.make_async_remote_copy(
@@ -104,62 +94,66 @@
         counter[t] += 1
         return send_sem.at[t, counter[t] - 1]
 
-    def hop(t, rel, to, device):
-        src = (shard.at[t] if rel == 0 else gs[t].at[0, rel]).at[own_part]
-        push(src, gs[t].at[0, to].at[own_part], token(t), ring_sem.at[t, to], (gx, device))
-
-    def spread(t, rel):
-        src = gs[t].at[0, rel]
-        push(src.at[out_part], src.at[out_part], token(t), side_sem.at[t, rel], (1 - gx, me))
-        push(src.at[own_part], gs[t].at[1, rel].at[own_part], token(t), pair_sem.at[t, rel], (gx, partner))
-
-    def cross(t, rel):
-        src = gs[t].at[0, rel].at[in_part]
-        arrived(src, side_sem.at[t, rel])
-        push(src, gs[t].at[1, rel].at[in_part], token(t), cross_sem.at[t, rel], (gx, partner))
-
-    def begin(t):
-        hop(t, 0, chips - 1, right)
-        hop(t, 0, 1, left)
-        push(shard.at[t], gs[t].at[1, 0], token(t), pair_sem.at[t, 0], (gx, partner))
-
-    def advance(t, k):
-        if k < half:
-            rel = chips - k
-            arrived(gs[t].at[0, rel].at[own_part], ring_sem.at[t, rel])
-            if k < half - 1 or t % 2 == 0:
-                hop(t, rel, rel - 1, right)
-            spread(t, rel)
-            arrived(gs[t].at[0, k].at[own_part], ring_sem.at[t, k])
-            if k < half - 1 or t % 2 == 1:
-                hop(t, k, k + 1, left)
-            spread(t, k)
-        else:
-            arrived(gs[t].at[0, half].at[own_part], ring_sem.at[t, half])
-            spread(t, half)
-        if k > 1:
-            cross(t, chips - k + 1)
-            cross(t, k - 1)
-        if k == half:
-            cross(t, half)
+    def send(t, src, dst, slot, device):
+        push(src, dst, token(t), gather_sem.at[t, slot], device)
+
+    def pair(t, row, levels, part, slot):
+        send(t, gs[t].at[0, row, levels, part], gs[t].at[1, row, levels, part], slot, (gx, partner))
+
+    def side(t, row, slot):
+        src = gs[t].at[0, row, far, ours]
+        send(t, src, src, slot, (1 - gx, me))
+
+    def launch(t):
+        for d in range(1, Z):
+            to = lax.rem(depth + d, Z) * 4 + lax.rem(me, 4)
+            send(t, shard.at[t, ours], gs[t].at[0, 0, Z - d, ours], 11 + Z - d, (gx, to))
+
+    def lead(t):
+        send(t, shard.at[t], gs[t].at[0, 1, 0], 0, (gx, across_y))
+        send(t, shard.at[t], gs[t].at[1, 0, 0], 5, (gx, partner))
+
+    def first(t):
+        for d in range(1, Z):
+            arrived(gs[t].at[0, 0, d, ours], gather_sem.at[t, 11 + d])
+        send(t, gs[t].at[0, 0, far, ours], gs[t].at[0, 1, far, ours], 1, (gx, across_y))
+        side(t, 0, 2)
+        pair(t, 0, far, ours, 6)
+        if t < 3:
+            lead(t + 1)
+
+    def second(t):
+        arrived(gs[t].at[0, 1, far, ours], gather_sem.at[t, 1])
+        side(t, 1, 3)
+        pair(t, 1, far, ours, 7)
+        arrived(gs[t].at[0, 1, 0], gather_sem.at[t, 0])
+        send(t, gs[t].at[0, 1, 0], gs[t].at[1, 1, 0], 8, (gx, partner))
+
+    def third(t):
+        arrived(gs[t].at[0, 0, far, theirs], gather_sem.at[t, 2])
+        pair(t, 0, far, theirs, 9)
+        arrived(gs[t].at[0, 1, far, theirs], gather_sem.at[t, 3])
+        pair(t, 1, far, theirs, 10)
 
     def settle(t):
-        arrived(gs[t].at[1, 0], pair_sem.at[t, 0])
-        for rel in range(1, chips):
-            arrived(gs[t].at[1, rel].at[own_part], pair_sem.at[t, rel])
-            arrived(gs[t].at[1, rel].at[in_part], cross_sem.at[t, rel])
+        arrived(gs[t].at[1, 0, 0], gather_sem.at[t, 5])
+        arrived(gs[t].at[1, 0, far, ours], gather_sem.at[t, 6])
+        arrived(gs[t].at[1, 1, far, ours], gather_sem.at[t, 7])
+        arrived(gs[t].at[1, 1, 0], gather_sem.at[t, 8])
+        arrived(gs[t].at[1, 0, far, theirs], gather_sem.at[t, 9])
+        arrived(gs[t].at[1, 1, far, theirs], gather_sem.at[t, 10])
 
     def load_tables(t):
         settle(t)
         g, w = gs[t], ws[t]
         for a in range(T):
             z, c, which = a // 4, (a // 2) % 2, a % 2
-            apos = z if c == 0 else chips - 1 - z
-            rel = lax.rem(apos - pos + chips, chips)
+            rel = lax.rem(z - depth + Z, Z)
+            row = jnp.where(col == c, 0, 1)
             other = jnp.where(core == which, 0, 1)
             for v in range(2):
                 for p in range(2):
-                    high, low = split(g[other, rel, 2 * v + p])
+                    high, low = split(g[other, row, rel, 2 * v + p])
                     rows = slice(a * K, (a + 1) * K)
                     cols = slice(p * CB, (p + 1) * CB)
                     w[v, 0, rows, cols] = high
@@ -202,35 +196,25 @@
                 pieces.append(ref[pl.ds(lo, rows, stride=CLO), :])
         return [jnp.concatenate([b[:, p * M:(p + 1) * M] for b in pieces], axis=1) for p in range(2)]
 
-    order = sorted(((t, k) for t in range(4) for k in range(half + 1)), key=lambda i: (i[1] + 1.1 * i[0], i[0]))
-    pending = []
-    for item in order:
-        if item[1] == 0:
-            begin(item[0])
-        elif item == (0, half):
-            advance(*item)
-            break
-        else:
-            advance(*item)
-    pending = list(order[order.index((0, half)) + 1:])
-
-    def more(count=1):
-        for _ in range(count):
-            if pending:
-                t, k = pending.pop(0)
-                if k == 0:
-                    begin(t)
-                else:
-                    advance(t, k)
-
     for t in range(4):
-        gs[t][0, 0] = shard[t]
+        launch(t)
+    lead(0)
+    pending = [(first, 0), (first, 1), (second, 0), (second, 1), (third, 0), (first, 2), (third, 1),
+               (first, 3), (second, 2), (second, 3), (third, 2), (third, 3)]
+
+    def more(count):
+        for _ in range(min(count, len(pending))):
+            action, t = pending.pop(0)
+            action(t)
+
+    more(5)
+    for t in range(4):
+        gs[t][0, 0, 0] = shard[t]
     load_tables(0)
     for s in range(S):
         y[s] = merge(0, values[s, 0], stem[s, 0], stem[s, 1])
-        more()
-    while any(t == 1 for t, k in pending):
-        more()
+        if s % 2:
+            more(1)
     load_tables(1)
     rows_of = lambda s, i: pl.ds(pl.multiple_of((s * T + i) * K, K), K)
     for s in range(S):
@@ -240,7 +224,7 @@
             to = lax.rem(me + d, T)
             push(sent.at[rows_of(s, to)], got.at[rows_of(s, me)], xs_sem.at[s, d], x_sem.at[s, d], (gx, to))
         got[rows_of(s, me), :] = sent[rows_of(s, me), :]
-        more()
+        more(1)
     more(len(pending))
     load_tables(2)
     load_tables(3)
@@ -316,7 +300,7 @@
     shard = jnp.take(branches, branch_order, axis=0).reshape(steps, 4, CB, K).transpose(0, 1, 3, 2)
     vmem = pl.BlockSpec(memory_space=pltpu.VMEM)
     dma = pltpu.SemaphoreType.DMA
-    table = pltpu.VMEM((2, T // 2, 4, K, CB), jnp.float32)
+    table = pltpu.VMEM((2, 2, T // 4, 4, K, CB), jnp.float32)
     merged = pltpu.VMEM((2, 2, CB, 2 * CB), jnp.bfloat16)
     moved = pltpu.VMEM((T * S * K, 2 * M), jnp.float32)
     gathered = pl.pallas_call(
@@ -332,8 +316,7 @@
             pltpu.VMEM((CB, 2 * M), jnp.float32),
             pltpu.VMEM((CB, 2 * M), jnp.float32),
             pltpu.VMEM((CB // (2 * M), 2 * M, 2 * M), jnp.float32),
-            dma((4, T // 2)), dma((4, T // 2)), dma((4, T // 2)), dma((4, T // 2)),
-            dma((4, 2 * T + 2)),
+            dma((4, 11 + T // 4)), dma((4, 11 + T // 4)),
             dma((S, T)), dma((T,)), dma((S, T)), dma((T,)),
         ],
         compiler_params=pltpu.CompilerParams(collective_id=0, has_side_effects=True),

time: 70.1 us -> 58.8 us (0.84)
  Pallas kernels: 63.9 us -> 52.6 us
    pallas_call x1, Pallas kernels: 63.9 us -> 52.6 us  [fused_device(): pl.pallas_call(functools.partial(kernel, (T, S, K, CB, M, CLO, CHI)), out...]
where the time goes in v3:
time: 58.8 us; the launch traced here: 58.6 us
  Pallas kernels  52.6 us (89%)
  local copies, waits for them, and re-layouts  3.82 us (6%)
  other arithmetic  2.15 us (4%)
    pallas_call x1, Pallas kernels, fused_device(): pl.pallas_call(functools.partial(kernel, (T, S, K, CB, M, CLO, CHI)), out...  52.6 us
    reshape x1, local copies, waits for them, and re-layouts, fused_device(): return gathered.reshape(2, entries)  1.67 us
    reshape x1, local copies, waits for them, and re-layouts, fused_device(): stem = stem_field.reshape(S, 2, M, CB)  1.23 us

profile of v3, /device:TPU:0, one launch (start us, length us, event | category | flops | bytes accessed | tf_op | source)
XLA Modules:
  0.0 58.6 jit_solution(9373881173495838418)
XLA Ops:
  0.0 0.0 copy-start
  0.0 0.7 %compare_and_fusion = pred[4]{0:T(512)(128)(4,1)S(1)} fusion(s32[4]{0:T(128)} %param.6), kind=kLoop, calls=%fused_computation.4 | loop fusion | flops 24 | bytes 20 | tf_op jit(solution)/shard_map/jit(_take)/and | solution.py:300
  0.7 0.7 %compare_select_fusion = s32[4]{0:T(128)S(1)} fusion(s32[4]{0:T(128)} %param.6), kind=kLoop, calls=%fused_computation.3 | loop fusion | flops 12 | bytes 32 | tf_op jit(solution)/shard_map/jit(_take)/jit(_where)/select_n | solution.py:300
  1.4 0.0 copy-done
  1.4 0.6 gather_fusion
  2.0 0.0 copy-start.1
  2.0 0.8 %select_bitcast_fusion.shard = f32[4,4,16,256]{3,2,1,0:T(8,128)} fusion(f32[4,4,256,16]{2,3,1,0:T(8,128)S(1)} %bitcast.3, pred[4]{0:T(512)(128)(4,1)S(1)} %compare_and_fusion), kind=kLoop, calls=%fused_computation.1 | loop fusion | flops 65536 | bytes 524292 | tf_op jit(solution)/shard_map/transpose | solution.py:300
  2.7 0.4 copy-done.1
  3.1 1.2 %reshape.13.stem = f32[4,2,64,256]{3,2,1,0:T(8,128)} reshape(f32[4,2,16384]{2,1,0:T(2,128)S(1)} %copy-done.1) | data formatting | bytes 1048576 | tf_op jit(solution)/shard_map/reshape | solution.py:299
  4.3 52.6 %shard_map.46 = f32[32,1024]{1,0:T(8,128)} custom-call(s32[4,4]{1,0:T(4,128)} %values.1, f32[4,2,64,256]{3,2,1,0:T(8,128)} %reshape.13.stem, f32[4,4,16,256]{3,2,1,0:T(8,128)} %select_bitcast_fusion.shard), custom_call_target="tpu_custom_call" | custom-call | tf_op jit(solution)/shard_map/pallas_call | solution.py:306
  56.9 1.7 %reshape.14 = f32[2,16384]{1,0:T(2,128)} reshape(f32[32,1024]{1,0:T(8,128)} %shard_map.46) | data formatting | bytes 262144 | tf_op jit(solution)/shard_map/reshape | solution.py:324
  (1 shorter events, 0.0 us)
Async XLA Ops:
  0.0 1.4 %copy-start = (f32[4,2,2,256,16]{3,4,2,1,0:T(8,128)S(1)}, f32[4,2,2,256,16]{3,4,2,1,0:T(8,128)}, u32[]{:S(2)}) copy-start(f32[4,2,2,256,16]{3,4,2,1,0:T(8,128)} %param.5) | copy-start | bytes 786436
  2.0 1.1 %copy-start.1 = (f32[4,2,16384]{2,1,0:T(2,128)S(1)}, f32[4,2,16384]{2,1,0:T(2,128)}, u32[]{:S(2)}) copy-start(f32[4,2,16384]{2,1,0:T(2,128)} %param.4) | copy-start | bytes 1572868

commit v4 on v3

--- a/solution.py
+++ b/solution.py
@@ -119,8 +119,8 @@
         send(t, gs[t].at[0, 0, far, ours], gs[t].at[0, 1, far, ours], 1, (gx, across_y))
         side(t, 0, 2)
         pair(t, 0, far, ours, 6)
-        if t < 3:
-            lead(t + 1)
+        if t < 2:
+            lead(t + 2)
 
     def second(t):
         arrived(gs[t].at[0, 1, far, ours], gather_sem.at[t, 1])
@@ -199,6 +199,7 @@
     for t in range(4):
         launch(t)
     lead(0)
+    lead(1)
     pending = [(first, 0), (first, 1), (second, 0), (second, 1), (third, 0), (first, 2), (third, 1),
                (first, 3), (second, 2), (second, 3), (third, 2), (third, 3)]
 
@@ -297,7 +298,7 @@
     CLO = CB // M
     CHI = K // CLO
     stem = stem_field.reshape(S, 2, M, CB)
-    shard = jnp.take(branches, branch_order, axis=0).reshape(steps, 4, CB, K).transpose(0, 1, 3, 2)
+    shard = branches.at[branch_order].get(mode="promise_in_bounds").reshape(steps, 4, CB, K).transpose(0, 1, 3, 2)
     vmem = pl.BlockSpec(memory_space=pltpu.VMEM)
     dma = pltpu.SemaphoreType.DMA
     table = pltpu.VMEM((2, 2, T // 4, 4, K, CB), jnp.float32)

time: 58.8 us -> 56.6 us (0.963)
  other arithmetic: 2.15 us -> 0.71 us
  Pallas kernels: 52.6 us -> 51.3 us
  local copies, waits for them, and re-layouts: 3.82 us -> 4.41 us
    pallas_call x1, Pallas kernels: 52.6 us -> 51.3 us  [fused_device(): pl.pallas_call(functools.partial(kernel, (T, S, K, CB, M, CLO, CHI)), out...]
    transpose x1 -> x0, other arithmetic: 0.78 us -> none  [fused_device(): jnp.take(branches, branch_order, axis=0).reshape(steps, 4, CB, K)]
    and x1 -> x0, other arithmetic: 0.7 us -> none  [fused_device(): jnp.take(branches, branch_order, axis=0).reshape(steps, 4, CB, K)]
    gather x1, local copies, waits for them, and re-layouts: 0.57 us -> 1.25 us  [fused_device(): branches.at[branch_order].get(mode='promise_in_bounds')]
where the time goes in v4:
time: 56.6 us; the launch traced here: 56.4 us
  Pallas kernels  51.3 us (91%)
  local copies, waits for them, and re-layouts  4.41 us (8%)
  other arithmetic  0.71 us (1%)
    pallas_call x1, Pallas kernels, fused_device(): pl.pallas_call(functools.partial(kernel, (T, S, K, CB, M, CLO, CHI)), out...  51.3 us
    reshape x1, local copies, waits for them, and re-layouts, fused_device(): return gathered.reshape(2, entries)  1.67 us
    gather x1, local copies, waits for them, and re-layouts, fused_device(): branches.at[branch_order].get(mode='promise_in_bounds')  1.25 us
    reshape x1, local copies, waits for them, and re-layouts, fused_device(): stem = stem_field.reshape(S, 2, M, CB)  1.23 us

profile of v4, /device:TPU:0, one launch (start us, length us, event | category | flops | bytes accessed | tf_op | source)
XLA Modules:
  0.0 56.4 jit_solution(4745249640859351686)
XLA Ops:
  0.0 0.0 copy-start
  0.0 0.7 %compare_select_fusion = s32[4]{0:T(128)S(1)} fusion(s32[4]{0:T(128)} %param.6), kind=kLoop, calls=%fused_computation.2 | loop fusion | flops 12 | bytes 32 | tf_op jit(solution)/shard_map/select_n | solution.py:301
  0.7 0.3 copy-done
  1.0 0.0 copy-start.1
  1.0 1.2 %gather_fusion = f32[4,2,2,256,16]{3,4,2,1,0:T(8,128)} fusion(f32[4,2,2,256,16]{3,4,2,1,0:T(8,128)S(1)} %copy-done, s32[1024]{0:T(1024)S(1)} %pad_clamp_fusion), kind=kCustom, calls=%fused_computation | custom fusion | bytes 524304 | tf_op jit(solution)/shard_map/gather | solution.py:301
  2.2 0.0 copy-done.1
  2.2 1.2 %reshape.9.stem = f32[4,2,64,256]{3,2,1,0:T(8,128)} reshape(f32[4,2,16384]{2,1,0:T(2,128)S(1)} %copy-done.1) | data formatting | bytes 1048576 | tf_op jit(solution)/shard_map/reshape | solution.py:300
  3.5 51.3 %shard_map.46 = f32[32,1024]{1,0:T(8,128)} custom-call(s32[4,4]{1,0:T(4,128)} %values.1, f32[4,2,64,256]{3,2,1,0:T(8,128)} %reshape.9.stem, f32[4,4,16,256]{3,2,1,0:T(8,128)} %bitcast.3), custom_call_target="tpu_custom_call" | custom-call | tf_op jit(solution)/shard_map/pallas_call | solution.py:307
  54.7 1.7 %reshape.11 = f32[2,16384]{1,0:T(2,128)} reshape(f32[32,1024]{1,0:T(8,128)} %shard_map.46) | data formatting | bytes 262144 | tf_op jit(solution)/shard_map/reshape | solution.py:325
  (1 shorter events, 0.0 us)
Async XLA Ops:
  0.0 1.0 %copy-start = (f32[4,2,2,256,16]{3,4,2,1,0:T(8,128)S(1)}, f32[4,2,2,256,16]{3,4,2,1,0:T(8,128)}, u32[]{:S(2)}) copy-start(f32[4,2,2,256,16]{3,4,2,1,0:T(8,128)} %param.5) | copy-start | bytes 786436
  1.0 1.3 %copy-start.1 = (f32[4,2,16384]{2,1,0:T(2,128)S(1)}, f32[4,2,16384]{2,1,0:T(2,128)}, u32[]{:S(2)}) copy-start(f32[4,2,16384]{2,1,0:T(2,128)} %param.4) | copy-start | bytes 1572868

commit v5 on v4

--- a/solution.py
+++ b/solution.py
@@ -120,6 +120,7 @@
         side(t, 0, 2)
         pair(t, 0, far, ours, 6)
         if t < 2:
+            launch(t + 2)
             lead(t + 2)
 
     def second(t):
@@ -196,7 +197,7 @@
                 pieces.append(ref[pl.ds(lo, rows, stride=CLO), :])
         return [jnp.concatenate([b[:, p * M:(p + 1) * M] for b in pieces], axis=1) for p in range(2)]
 
-    for t in range(4):
+    for t in range(2):
         launch(t)
     lead(0)
     lead(1)

time: 56.6 us -> 55.1 us (0.973)
  Pallas kernels: 51.3 us -> 49.8 us
    pallas_call x1, Pallas kernels: 51.3 us -> 49.8 us  [fused_device(): pl.pallas_call(functools.partial(kernel, (T, S, K, CB, M, CLO, CHI)), out...]
where the time goes in v5:
time: 55.1 us; the launch traced here: 55 us
  Pallas kernels  49.8 us (90%)
  local copies, waits for them, and re-layouts  4.41 us (8%)
  other arithmetic  0.71 us (1%)
    pallas_call x1, Pallas kernels, fused_device(): pl.pallas_call(functools.partial(kernel, (T, S, K, CB, M, CLO, CHI)), out...  49.8 us
    reshape x1, local copies, waits for them, and re-layouts, fused_device(): return gathered.reshape(2, entries)  1.67 us
    gather x1, local copies, waits for them, and re-layouts, fused_device(): branches.at[branch_order].get(mode='promise_in_bounds')  1.25 us
    reshape x1, local copies, waits for them, and re-layouts, fused_device(): stem = stem_field.reshape(S, 2, M, CB)  1.23 us

profile of v5, /device:TPU:0, one launch (start us, length us, event | category | flops | bytes accessed | tf_op | source)
XLA Modules:
  0.0 55.0 jit_solution(1221769379140632125)
XLA Ops:
  0.0 0.0 copy-start
  0.0 0.7 %compare_select_fusion = s32[4]{0:T(128)S(1)} fusion(s32[4]{0:T(128)} %param.6), kind=kLoop, calls=%fused_computation.2 | loop fusion | flops 12 | bytes 32 | tf_op jit(solution)/shard_map/select_n | solution.py:302
  0.7 0.3 copy-done
  1.0 0.0 copy-start.1
  1.0 1.2 %gather_fusion = f32[4,2,2,256,16]{3,4,2,1,0:T(8,128)} fusion(f32[4,2,2,256,16]{3,4,2,1,0:T(8,128)S(1)} %copy-done, s32[1024]{0:T(1024)S(1)} %pad_clamp_fusion), kind=kCustom, calls=%fused_computation | custom fusion | bytes 524304 | tf_op jit(solution)/shard_map/gather | solution.py:302
  2.2 0.0 copy-done.1
  2.2 1.2 %reshape.9.stem = f32[4,2,64,256]{3,2,1,0:T(8,128)} reshape(f32[4,2,16384]{2,1,0:T(2,128)S(1)} %copy-done.1) | data formatting | bytes 1048576 | tf_op jit(solution)/shard_map/reshape | solution.py:301
  3.5 49.8 %shard_map.46 = f32[32,1024]{1,0:T(8,128)} custom-call(s32[4,4]{1,0:T(4,128)} %values.1, f32[4,2,64,256]{3,2,1,0:T(8,128)} %reshape.9.stem, f32[4,4,16,256]{3,2,1,0:T(8,128)} %bitcast.3), custom_call_target="tpu_custom_call" | custom-call | tf_op jit(solution)/shard_map/pallas_call | solution.py:308
  53.3 1.7 %reshape.11 = f32[2,16384]{1,0:T(2,128)} reshape(f32[32,1024]{1,0:T(8,128)} %shard_map.46) | data formatting | bytes 262144 | tf_op jit(solution)/shard_map/reshape | solution.py:326
  (1 shorter events, 0.0 us)
Async XLA Ops:
  0.0 1.0 %copy-start = (f32[4,2,2,256,16]{3,4,2,1,0:T(8,128)S(1)}, f32[4,2,2,256,16]{3,4,2,1,0:T(8,128)}, u32[]{:S(2)}) copy-start(f32[4,2,2,256,16]{3,4,2,1,0:T(8,128)} %param.5) | copy-start | bytes 786436
  1.0 1.3 %copy-start.1 = (f32[4,2,16384]{2,1,0:T(2,128)S(1)}, f32[4,2,16384]{2,1,0:T(2,128)}, u32[]{:S(2)}) copy-start(f32[4,2,16384]{2,1,0:T(2,128)} %param.4) | copy-start | bytes 1572868
